TPU v7x, 32 devices: a whole 2x2x4 slice. The times are simulated.
32 devices in a mesh: row: 4 (over z), col: 8 (over y, x, core).
Axes of the slice: x: 2, y: 2, z: 4, core: 2. Of those that a mesh axis runs over, the one named last changes fastest.
Arguments:
- adjacency: int32 [32768, 2048], P('col', 'row'), may hold values from -2147483648 to 2147483647, as said below
- frontier: bfloat16 [65536, 128], P(('row', 'col')), may hold values from 0 to 1, as said below
- visited: int32 [4, 32768], P(None, ('col', 'row')), may hold values from -2147483648 to 2147483647, as said below
Outputs:
- path_counts: float32 [32768, 128], P(('col', 'row'))
- reached_bits: int32 [4, 32768], P(None, ('col', 'row'))
Inputs may be any that keep to these rules, and one draw needn't show every extreme that they name: Bit k of adjacency[d, w] is the edge from source vertex 32 w + k to destination d; degrees and edge densities differ between vertices and between blocks of 128 by 128 vertices. `frontier`: values are zero or between 0.1 and 1. Bit k of visited[w, d] tells whether destination d was reached from root 32 w + k.
All inputs are finite; a program needn't handle non-finite values.
Results may differ from a plain program's by a relative error of at most 0.0003.
Values may be sent and summed in bfloat16 or wider, within the bound.
A program may use at most 64 MiB of HBM per device.

v0:
```python
import functools
import math
import jax
import jax.numpy as jnp
from jax import lax
from jax.sharding import PartitionSpec as P


def expand_bits(packed):
    shift_table = jnp.arange(32, dtype=jnp.int32)
    bit_table = jnp.bitwise_and(jnp.right_shift(packed[:, :, None], shift_table), 1)
    return bit_table.reshape(packed.shape[0], packed.shape[1] * 32).astype(jnp.bfloat16)


def tile_product(packed, vectors):
    row_total = packed.shape[0]
    src_width = vectors.shape[0]
    row_len = math.gcd(row_total, 1024)
    block_len = math.gcd(src_width, 4096)
    block_count = src_width // block_len
    row_blocks = packed.reshape(row_total // row_len, row_len, packed.shape[1])

    def one_rows(packed_rows):
        initial = jnp.zeros((row_len, vectors.shape[1]), jnp.float32)

        def add_block(turn_index, total):
            offset = turn_index * block_len
            packed_cols = lax.dynamic_slice_in_dim(packed_rows, offset // 32, block_len // 32, 1)
            vector_rows = lax.dynamic_slice_in_dim(vectors, offset, block_len, 0)
            return total + jnp.dot(
                expand_bits(packed_cols), vector_rows, preferred_element_type=jnp.float32
            )

        return lax.fori_loop(0, block_count, add_block, initial)

    return lax.map(one_rows, row_blocks).reshape(row_total, vectors.shape[1])


def finish(reached, visited):
    row_count = reached.shape[0]
    word_count = visited.shape[0]
    shift_table = jnp.arange(32, dtype=jnp.int32)
    seen_bits = jnp.bitwise_and(jnp.right_shift(visited[:, :, None], shift_table), 1)
    seen_bits = jnp.transpose(seen_bits, (1, 0, 2)).reshape(row_count, word_count * 32)
    path_counts = jnp.where(seen_bits == 1, jnp.float32(0.0), reached)
    fresh = jnp.logical_and(seen_bits == 0, reached > 0).astype(jnp.int32)
    fresh = fresh.reshape(row_count, word_count, 32)
    added = functools.reduce(
        jnp.bitwise_or, [jnp.left_shift(fresh[:, :, position], position) for position in range(32)]
    )
    reached_bits = jnp.bitwise_or(visited, jnp.transpose(added))
    return (path_counts, reached_bits)


def shards(adjacency, frontier, visited):
    partial_sum = tile_product(adjacency, lax.all_gather(frontier, "col", axis=0, tiled=True))
    reached = lax.psum_scatter(partial_sum, "row", scatter_dimension=0, tiled=True)
    return finish(reached, visited)


def solution(mesh):
    placed = (P("col", "row"), P(("row", "col"), None), P(None, ("col", "row")))
    return jax.shard_map(
        shards,
        mesh=mesh,
        in_specs=placed,
        out_specs=(P(("col", "row"), None), P(None, ("col", "row"))),
        check_vma=False,
    )
```

profile of v0, /device:TPU:0, one launch (start us, length us, event | category | flops | bytes accessed | tf_op | source)
XLA Modules:
  0.0 302.6 jit_solution(3641786768029354774)
XLA Ops:
  8.0 41.2 %all-gather.2.cloned.1.call-done = bf16[16384,128]{1,0:T(8,128)(2,1)} async-done(((bf16[2048,128]{1,0:T(8,128)(2,1)}), bf16[16384,128]{1,0:T(8,128)(2,1)}) %all-gather.2.cloned.1.call-update) | async-done | bytes 4194320 | tf_op jit(solution)/shard_map/all_gather | solution.py:56
  49.2 195.2 %while.36 = (s32[]{:T(128)}, f32[4,1024,128]{2,1,0:T(8,128)}, s32[4,1024,512]{2,1,0:T(8,128)}, bf16[16384,128]{1,0:T(8,128)(2,1)}, s32[]{:T(128)}, /*index=5*/s3...) while((s32[]{:T(128)}, f32[4,1024,128]{2,1,0:T(8,128)}, ...), condition=%wide.region_3.4_spmd, body=%wide.region_0.3_spmd.sunk | while | flops 1086586880 | bytes 29951060 | solution.py:36
  49.2 3.1 %constant_dynamic-slice_fusion.4 = s32[1,1024,512]{2,1,0:T(8,128)} fusion(s32[4,1024,512]{2,1,0:T(8,128)} %get-tuple-element.379, s32[]{:T(128)} %get-tuple-element.363), kind=kLoop, calls=%fused_computation.8.clone.1 | loop fusion | bytes 4194308 | tf_op jit(solution)/shard_map/while/body/jit(dynamic_index_in_dim)/dynamic_slice | solution.py:36
  52.3 1.9 copy.298
  54.2 42.9 %while.37 = (s32[]{:T(128)}, f32[1024,128]{1,0:T(8,128)S(1)}, s32[1024,512]{0,1:T(8,128)S(1)}, bf16[16384,128]{1,0:T(8,128)(2,1)}, s32[]{:T(128)}, /*index=5*/s3...) while((s32[]{:T(128)}, f32[1024,128]{1,0:T(8,128)S(1)}, ...), condition=%wide.region_2.2_spmd.clone, body=%wide.region_1.1_spmd.clone.sunk | while | flops 1086586880 | bytes 20513124 | solution.py:34
  54.4 4.4 %fusion.66 = bf16[1024,4096]{0,1:T(8,128)(2,1)} fusion(s32[4096]{0:T(1024)S(1)} %shift_right_arithmetic.108, s32[1024,128]{0,1:T(8,128)S(1)} %constant_dynamic-slice_fusion.5), kind=kLoop, calls=%fused_computation.2.clone.1 | loop fusion | flops 12582912 | bytes 8929280 | tf_op jit(solution)/shard_map/while/body/eval_jaxpr/while/body/eval_jaxpr/convert_element_type | solution.py:12
  58.9 6.1 %convolution_add_fusion.2 = f32[1024,128]{1,0:T(8,128)S(1)} fusion(bf16[1024,4096]{0,1:T(8,128)(2,1)} %fusion.66, bf16[16384,128]{1,0:T(8,128)(2,1)} %get-tuple-element.340, s32[]{:T(128)S(6)} %select_n.46, f32[1024,128]{1,0:T(8,128)S(1)} %get-tuple-element.326, pred[]{:T(512)S(6)} %compare.13), kind=kOutput, calls=%fused_computation.3.clone.1 | convolution fusion | flops 1074003968 | bytes 10485765 | tf_op jit(solution)/shard_map/while/body/eval_jaxpr/while/body/eval_jaxpr/dot_general | solution.py:30
  65.2 4.4 %fusion.66 = bf16[1024,4096]{0,1:T(8,128)(2,1)} fusion(s32[4096]{0:T(1024)S(1)} %shift_right_arithmetic.108, s32[1024,128]{0,1:T(8,128)S(1)} %constant_dynamic-slice_fusion.5), kind=kLoop, calls=%fused_computation.2.clone.1 | loop fusion | flops 12582912 | bytes 8929280 | tf_op jit(solution)/shard_map/while/body/eval_jaxpr/while/body/eval_jaxpr/convert_element_type | solution.py:12
  69.6 6.1 %convolution_add_fusion.2 = f32[1024,128]{1,0:T(8,128)S(1)} fusion(bf16[1024,4096]{0,1:T(8,128)(2,1)} %fusion.66, bf16[16384,128]{1,0:T(8,128)(2,1)} %get-tuple-element.340, s32[]{:T(128)S(6)} %select_n.46, f32[1024,128]{1,0:T(8,128)S(1)} %get-tuple-element.326, pred[]{:T(512)S(6)} %compare.13), kind=kOutput, calls=%fused_computation.3.clone.1 | convolution fusion | flops 1074003968 | bytes 10485765 | tf_op jit(solution)/shard_map/while/body/eval_jaxpr/while/body/eval_jaxpr/dot_general | solution.py:30
  75.9 4.4 %fusion.66 = bf16[1024,4096]{0,1:T(8,128)(2,1)} fusion(s32[4096]{0:T(1024)S(1)} %shift_right_arithmetic.108, s32[1024,128]{0,1:T(8,128)S(1)} %constant_dynamic-slice_fusion.5), kind=kLoop, calls=%fused_computation.2.clone.1 | loop fusion | flops 12582912 | bytes 8929280 | tf_op jit(solution)/shard_map/while/body/eval_jaxpr/while/body/eval_jaxpr/convert_element_type | solution.py:12
  80.3 6.1 %convolution_add_fusion.2 = f32[1024,128]{1,0:T(8,128)S(1)} fusion(bf16[1024,4096]{0,1:T(8,128)(2,1)} %fusion.66, bf16[16384,128]{1,0:T(8,128)(2,1)} %get-tuple-element.340, s32[]{:T(128)S(6)} %select_n.46, f32[1024,128]{1,0:T(8,128)S(1)} %get-tuple-element.326, pred[]{:T(512)S(6)} %compare.13), kind=kOutput, calls=%fused_computation.3.clone.1 | convolution fusion | flops 1074003968 | bytes 10485765 | tf_op jit(solution)/shard_map/while/body/eval_jaxpr/while/body/eval_jaxpr/dot_general | solution.py:30
  86.6 4.4 %fusion.66 = bf16[1024,4096]{0,1:T(8,128)(2,1)} fusion(s32[4096]{0:T(1024)S(1)} %shift_right_arithmetic.108, s32[1024,128]{0,1:T(8,128)S(1)} %constant_dynamic-slice_fusion.5), kind=kLoop, calls=%fused_computation.2.clone.1 | loop fusion | flops 12582912 | bytes 8929280 | tf_op jit(solution)/shard_map/while/body/eval_jaxpr/while/body/eval_jaxpr/convert_element_type | solution.py:12
  91.1 6.1 %convolution_add_fusion.2 = f32[1024,128]{1,0:T(8,128)S(1)} fusion(bf16[1024,4096]{0,1:T(8,128)(2,1)} %fusion.66, bf16[16384,128]{1,0:T(8,128)(2,1)} %get-tuple-element.340, s32[]{:T(128)S(6)} %select_n.46, f32[1024,128]{1,0:T(8,128)S(1)} %get-tuple-element.326, pred[]{:T(512)S(6)} %compare.13), kind=kOutput, calls=%fused_computation.3.clone.1 | convolution fusion | flops 1074003968 | bytes 10485765 | tf_op jit(solution)/shard_map/while/body/eval_jaxpr/while/body/eval_jaxpr/dot_general | solution.py:30
  98.0 3.1 %constant_dynamic-slice_fusion.4 = s32[1,1024,512]{2,1,0:T(8,128)} fusion(s32[4,1024,512]{2,1,0:T(8,128)} %get-tuple-element.379, s32[]{:T(128)} %get-tuple-element.363), kind=kLoop, calls=%fused_computation.8.clone.1 | loop fusion | bytes 4194308 | tf_op jit(solution)/shard_map/while/body/jit(dynamic_index_in_dim)/dynamic_slice | solution.py:36
  101.1 1.9 copy.298
  103.1 42.9 %while.37 = (s32[]{:T(128)}, f32[1024,128]{1,0:T(8,128)S(1)}, s32[1024,512]{0,1:T(8,128)S(1)}, bf16[16384,128]{1,0:T(8,128)(2,1)}, s32[]{:T(128)}, /*index=5*/s3...) while((s32[]{:T(128)}, f32[1024,128]{1,0:T(8,128)S(1)}, ...), condition=%wide.region_2.2_spmd.clone, body=%wide.region_1.1_spmd.clone.sunk | while | flops 1086586880 | bytes 20513124 | solution.py:34
  103.3 4.4 %fusion.66 = bf16[1024,4096]{0,1:T(8,128)(2,1)} fusion(s32[4096]{0:T(1024)S(1)} %shift_right_arithmetic.108, s32[1024,128]{0,1:T(8,128)S(1)} %constant_dynamic-slice_fusion.5), kind=kLoop, calls=%fused_computation.2.clone.1 | loop fusion | flops 12582912 | bytes 8929280 | tf_op jit(solution)/shard_map/while/body/eval_jaxpr/while/body/eval_jaxpr/convert_element_type | solution.py:12
  107.7 6.1 %convolution_add_fusion.2 = f32[1024,128]{1,0:T(8,128)S(1)} fusion(bf16[1024,4096]{0,1:T(8,128)(2,1)} %fusion.66, bf16[16384,128]{1,0:T(8,128)(2,1)} %get-tuple-element.340, s32[]{:T(128)S(6)} %select_n.46, f32[1024,128]{1,0:T(8,128)S(1)} %get-tuple-element.326, pred[]{:T(512)S(6)} %compare.13), kind=kOutput, calls=%fused_computation.3.clone.1 | convolution fusion | flops 1074003968 | bytes 10485765 | tf_op jit(solution)/shard_map/while/body/eval_jaxpr/while/body/eval_jaxpr/dot_general | solution.py:30
  114.0 4.4 %fusion.66 = bf16[1024,4096]{0,1:T(8,128)(2,1)} fusion(s32[4096]{0:T(1024)S(1)} %shift_right_arithmetic.108, s32[1024,128]{0,1:T(8,128)S(1)} %constant_dynamic-slice_fusion.5), kind=kLoop, calls=%fused_computation.2.clone.1 | loop fusion | flops 12582912 | bytes 8929280 | tf_op jit(solution)/shard_map/while/body/eval_jaxpr/while/body/eval_jaxpr/convert_element_type | solution.py:12
  118.4 6.1 %convolution_add_fusion.2 = f32[1024,128]{1,0:T(8,128)S(1)} fusion(bf16[1024,4096]{0,1:T(8,128)(2,1)} %fusion.66, bf16[16384,128]{1,0:T(8,128)(2,1)} %get-tuple-element.340, s32[]{:T(128)S(6)} %select_n.46, f32[1024,128]{1,0:T(8,128)S(1)} %get-tuple-element.326, pred[]{:T(512)S(6)} %compare.13), kind=kOutput, calls=%fused_computation.3.clone.1 | convolution fusion | flops 1074003968 | bytes 10485765 | tf_op jit(solution)/shard_map/while/body/eval_jaxpr/while/body/eval_jaxpr/dot_general | solution.py:30
  124.7 4.4 %fusion.66 = bf16[1024,4096]{0,1:T(8,128)(2,1)} fusion(s32[4096]{0:T(1024)S(1)} %shift_right_arithmetic.108, s32[1024,128]{0,1:T(8,128)S(1)} %constant_dynamic-slice_fusion.5), kind=kLoop, calls=%fused_computation.2.clone.1 | loop fusion | flops 12582912 | bytes 8929280 | tf_op jit(solution)/shard_map/while/body/eval_jaxpr/while/body/eval_jaxpr/convert_element_type | solution.py:12
  129.2 6.1 %convolution_add_fusion.2 = f32[1024,128]{1,0:T(8,128)S(1)} fusion(bf16[1024,4096]{0,1:T(8,128)(2,1)} %fusion.66, bf16[16384,128]{1,0:T(8,128)(2,1)} %get-tuple-element.340, s32[]{:T(128)S(6)} %select_n.46, f32[1024,128]{1,0:T(8,128)S(1)} %get-tuple-element.326, pred[]{:T(512)S(6)} %compare.13), kind=kOutput, calls=%fused_computation.3.clone.1 | convolution fusion | flops 1074003968 | bytes 10485765 | tf_op jit(solution)/shard_map/while/body/eval_jaxpr/while/body/eval_jaxpr/dot_general | solution.py:30
  135.5 4.4 %fusion.66 = bf16[1024,4096]{0,1:T(8,128)(2,1)} fusion(s32[4096]{0:T(1024)S(1)} %shift_right_arithmetic.108, s32[1024,128]{0,1:T(8,128)S(1)} %constant_dynamic-slice_fusion.5), kind=kLoop, calls=%fused_computation.2.clone.1 | loop fusion | flops 12582912 | bytes 8929280 | tf_op jit(solution)/shard_map/while/body/eval_jaxpr/while/body/eval_jaxpr/convert_element_type | solution.py:12
  139.9 6.1 %convolution_add_fusion.2 = f32[1024,128]{1,0:T(8,128)S(1)} fusion(bf16[1024,4096]{0,1:T(8,128)(2,1)} %fusion.66, bf16[16384,128]{1,0:T(8,128)(2,1)} %get-tuple-element.340, s32[]{:T(128)S(6)} %select_n.46, f32[1024,128]{1,0:T(8,128)S(1)} %get-tuple-element.326, pred[]{:T(512)S(6)} %compare.13), kind=kOutput, calls=%fused_computation.3.clone.1 | convolution fusion | flops 1074003968 | bytes 10485765 | tf_op jit(solution)/shard_map/while/body/eval_jaxpr/while/body/eval_jaxpr/dot_general | solution.py:30
  146.8 3.1 %constant_dynamic-slice_fusion.4 = s32[1,1024,512]{2,1,0:T(8,128)} fusion(s32[4,1024,512]{2,1,0:T(8,128)} %get-tuple-element.379, s32[]{:T(128)} %get-tuple-element.363), kind=kLoop, calls=%fused_computation.8.clone.1 | loop fusion | bytes 4194308 | tf_op jit(solution)/shard_map/while/body/jit(dynamic_index_in_dim)/dynamic_slice | solution.py:36
  150.0 1.9 copy.298
  151.9 42.9 %while.37 = (s32[]{:T(128)}, f32[1024,128]{1,0:T(8,128)S(1)}, s32[1024,512]{0,1:T(8,128)S(1)}, bf16[16384,128]{1,0:T(8,128)(2,1)}, s32[]{:T(128)}, /*index=5*/s3...) while((s32[]{:T(128)}, f32[1024,128]{1,0:T(8,128)S(1)}, ...), condition=%wide.region_2.2_spmd.clone, body=%wide.region_1.1_spmd.clone.sunk | while | flops 1086586880 | bytes 20513124 | solution.py:34
  152.1 4.4 %fusion.66 = bf16[1024,4096]{0,1:T(8,128)(2,1)} fusion(s32[4096]{0:T(1024)S(1)} %shift_right_arithmetic.108, s32[1024,128]{0,1:T(8,128)S(1)} %constant_dynamic-slice_fusion.5), kind=kLoop, calls=%fused_computation.2.clone.1 | loop fusion | flops 12582912 | bytes 8929280 | tf_op jit(solution)/shard_map/while/body/eval_jaxpr/while/body/eval_jaxpr/convert_element_type | solution.py:12
  156.5 6.1 %convolution_add_fusion.2 = f32[1024,128]{1,0:T(8,128)S(1)} fusion(bf16[1024,4096]{0,1:T(8,128)(2,1)} %fusion.66, bf16[16384,128]{1,0:T(8,128)(2,1)} %get-tuple-element.340, s32[]{:T(128)S(6)} %select_n.46, f32[1024,128]{1,0:T(8,128)S(1)} %get-tuple-element.326, pred[]{:T(512)S(6)} %compare.13), kind=kOutput, calls=%fused_computation.3.clone.1 | convolution fusion | flops 1074003968 | bytes 10485765 | tf_op jit(solution)/shard_map/while/body/eval_jaxpr/while/body/eval_jaxpr/dot_general | solution.py:30
  162.8 4.4 %fusion.66 = bf16[1024,4096]{0,1:T(8,128)(2,1)} fusion(s32[4096]{0:T(1024)S(1)} %shift_right_arithmetic.108, s32[1024,128]{0,1:T(8,128)S(1)} %constant_dynamic-slice_fusion.5), kind=kLoop, calls=%fused_computation.2.clone.1 | loop fusion | flops 12582912 | bytes 8929280 | tf_op jit(solution)/shard_map/while/body/eval_jaxpr/while/body/eval_jaxpr/convert_element_type | solution.py:12
  167.2 6.1 %convolution_add_fusion.2 = f32[1024,128]{1,0:T(8,128)S(1)} fusion(bf16[1024,4096]{0,1:T(8,128)(2,1)} %fusion.66, bf16[16384,128]{1,0:T(8,128)(2,1)} %get-tuple-element.340, s32[]{:T(128)S(6)} %select_n.46, f32[1024,128]{1,0:T(8,128)S(1)} %get-tuple-element.326, pred[]{:T(512)S(6)} %compare.13), kind=kOutput, calls=%fused_computation.3.clone.1 | convolution fusion | flops 1074003968 | bytes 10485765 | tf_op jit(solution)/shard_map/while/body/eval_jaxpr/while/body/eval_jaxpr/dot_general | solution.py:30
  173.5 4.4 %fusion.66 = bf16[1024,4096]{0,1:T(8,128)(2,1)} fusion(s32[4096]{0:T(1024)S(1)} %shift_right_arithmetic.108, s32[1024,128]{0,1:T(8,128)S(1)} %constant_dynamic-slice_fusion.5), kind=kLoop, calls=%fused_computation.2.clone.1 | loop fusion | flops 12582912 | bytes 8929280 | tf_op jit(solution)/shard_map/while/body/eval_jaxpr/while/body/eval_jaxpr/convert_element_type | solution.py:12
  178.0 6.1 %convolution_add_fusion.2 = f32[1024,128]{1,0:T(8,128)S(1)} fusion(bf16[1024,4096]{0,1:T(8,128)(2,1)} %fusion.66, bf16[16384,128]{1,0:T(8,128)(2,1)} %get-tuple-element.340, s32[]{:T(128)S(6)} %select_n.46, f32[1024,128]{1,0:T(8,128)S(1)} %get-tuple-element.326, pred[]{:T(512)S(6)} %compare.13), kind=kOutput, calls=%fused_computation.3.clone.1 | convolution fusion | flops 1074003968 | bytes 10485765 | tf_op jit(solution)/shard_map/while/body/eval_jaxpr/while/body/eval_jaxpr/dot_general | solution.py:30
  184.3 4.4 %fusion.66 = bf16[1024,4096]{0,1:T(8,128)(2,1)} fusion(s32[4096]{0:T(1024)S(1)} %shift_right_arithmetic.108, s32[1024,128]{0,1:T(8,128)S(1)} %constant_dynamic-slice_fusion.5), kind=kLoop, calls=%fused_computation.2.clone.1 | loop fusion | flops 12582912 | bytes 8929280 | tf_op jit(solution)/shard_map/while/body/eval_jaxpr/while/body/eval_jaxpr/convert_element_type | solution.py:12
  188.7 6.1 %convolution_add_fusion.2 = f32[1024,128]{1,0:T(8,128)S(1)} fusion(bf16[1024,4096]{0,1:T(8,128)(2,1)} %fusion.66, bf16[16384,128]{1,0:T(8,128)(2,1)} %get-tuple-element.340, s32[]{:T(128)S(6)} %select_n.46, f32[1024,128]{1,0:T(8,128)S(1)} %get-tuple-element.326, pred[]{:T(512)S(6)} %compare.13), kind=kOutput, calls=%fused_computation.3.clone.1 | convolution fusion | flops 1074003968 | bytes 10485765 | tf_op jit(solution)/shard_map/while/body/eval_jaxpr/while/body/eval_jaxpr/dot_general | solution.py:30
  195.7 3.1 %constant_dynamic-slice_fusion.4 = s32[1,1024,512]{2,1,0:T(8,128)} fusion(s32[4,1024,512]{2,1,0:T(8,128)} %get-tuple-element.379, s32[]{:T(128)} %get-tuple-element.363), kind=kLoop, calls=%fused_computation.8.clone.1 | loop fusion | bytes 4194308 | tf_op jit(solution)/shard_map/while/body/jit(dynamic_index_in_dim)/dynamic_slice | solution.py:36
  198.8 1.9 copy.298
  200.7 42.9 %while.37 = (s32[]{:T(128)}, f32[1024,128]{1,0:T(8,128)S(1)}, s32[1024,512]{0,1:T(8,128)S(1)}, bf16[16384,128]{1,0:T(8,128)(2,1)}, s32[]{:T(128)}, /*index=5*/s3...) while((s32[]{:T(128)}, f32[1024,128]{1,0:T(8,128)S(1)}, ...), condition=%wide.region_2.2_spmd.clone, body=%wide.region_1.1_spmd.clone.sunk | while | flops 1086586880 | bytes 20513124 | solution.py:34
  200.9 4.4 %fusion.66 = bf16[1024,4096]{0,1:T(8,128)(2,1)} fusion(s32[4096]{0:T(1024)S(1)} %shift_right_arithmetic.108, s32[1024,128]{0,1:T(8,128)S(1)} %constant_dynamic-slice_fusion.5), kind=kLoop, calls=%fused_computation.2.clone.1 | loop fusion | flops 12582912 | bytes 8929280 | tf_op jit(solution)/shard_map/while/body/eval_jaxpr/while/body/eval_jaxpr/convert_element_type | solution.py:12
  205.3 6.1 %convolution_add_fusion.2 = f32[1024,128]{1,0:T(8,128)S(1)} fusion(bf16[1024,4096]{0,1:T(8,128)(2,1)} %fusion.66, bf16[16384,128]{1,0:T(8,128)(2,1)} %get-tuple-element.340, s32[]{:T(128)S(6)} %select_n.46, f32[1024,128]{1,0:T(8,128)S(1)} %get-tuple-element.326, pred[]{:T(512)S(6)} %compare.13), kind=kOutput, calls=%fused_computation.3.clone.1 | convolution fusion | flops 1074003968 | bytes 10485765 | tf_op jit(solution)/shard_map/while/body/eval_jaxpr/while/body/eval_jaxpr/dot_general | solution.py:30
  211.6 4.4 %fusion.66 = bf16[1024,4096]{0,1:T(8,128)(2,1)} fusion(s32[4096]{0:T(1024)S(1)} %shift_right_arithmetic.108, s32[1024,128]{0,1:T(8,128)S(1)} %constant_dynamic-slice_fusion.5), kind=kLoop, calls=%fused_computation.2.clone.1 | loop fusion | flops 12582912 | bytes 8929280 | tf_op jit(solution)/shard_map/while/body/eval_jaxpr/while/body/eval_jaxpr/convert_element_type | solution.py:12
  216.1 6.1 %convolution_add_fusion.2 = f32[1024,128]{1,0:T(8,128)S(1)} fusion(bf16[1024,4096]{0,1:T(8,128)(2,1)} %fusion.66, bf16[16384,128]{1,0:T(8,128)(2,1)} %get-tuple-element.340, s32[]{:T(128)S(6)} %select_n.46, f32[1024,128]{1,0:T(8,128)S(1)} %get-tuple-element.326, pred[]{:T(512)S(6)} %compare.13), kind=kOutput, calls=%fused_computation.3.clone.1 | convolution fusion | flops 1074003968 | bytes 10485765 | tf_op jit(solution)/shard_map/while/body/eval_jaxpr/while/body/eval_jaxpr/dot_general | solution.py:30
  222.4 4.4 %fusion.66 = bf16[1024,4096]{0,1:T(8,128)(2,1)} fusion(s32[4096]{0:T(1024)S(1)} %shift_right_arithmetic.108, s32[1024,128]{0,1:T(8,128)S(1)} %constant_dynamic-slice_fusion.5), kind=kLoop, calls=%fused_computation.2.clone.1 | loop fusion | flops 12582912 | bytes 8929280 | tf_op jit(solution)/shard_map/while/body/eval_jaxpr/while/body/eval_jaxpr/convert_element_type | solution.py:12
  226.8 6.1 %convolution_add_fusion.2 = f32[1024,128]{1,0:T(8,128)S(1)} fusion(bf16[1024,4096]{0,1:T(8,128)(2,1)} %fusion.66, bf16[16384,128]{1,0:T(8,128)(2,1)} %get-tuple-element.340, s32[]{:T(128)S(6)} %select_n.46, f32[1024,128]{1,0:T(8,128)S(1)} %get-tuple-element.326, pred[]{:T(512)S(6)} %compare.13), kind=kOutput, calls=%fused_computation.3.clone.1 | convolution fusion | flops 1074003968 | bytes 10485765 | tf_op jit(solution)/shard_map/while/body/eval_jaxpr/while/body/eval_jaxpr/dot_general | solution.py:30
  233.1 4.4 %fusion.66 = bf16[1024,4096]{0,1:T(8,128)(2,1)} fusion(s32[4096]{0:T(1024)S(1)} %shift_right_arithmetic.108, s32[1024,128]{0,1:T(8,128)S(1)} %constant_dynamic-slice_fusion.5), kind=kLoop, calls=%fused_computation.2.clone.1 | loop fusion | flops 12582912 | bytes 8929280 | tf_op jit(solution)/shard_map/while/body/eval_jaxpr/while/body/eval_jaxpr/convert_element_type | solution.py:12
  237.5 6.1 %convolution_add_fusion.2 = f32[1024,128]{1,0:T(8,128)S(1)} fusion(bf16[1024,4096]{0,1:T(8,128)(2,1)} %fusion.66, bf16[16384,128]{1,0:T(8,128)(2,1)} %get-tuple-element.340, s32[]{:T(128)S(6)} %select_n.46, f32[1024,128]{1,0:T(8,128)S(1)} %get-tuple-element.326, pred[]{:T(512)S(6)} %compare.13), kind=kOutput, calls=%fused_computation.3.clone.1 | convolution fusion | flops 1074003968 | bytes 10485765 | tf_op jit(solution)/shard_map/while/body/eval_jaxpr/while/body/eval_jaxpr/dot_general | solution.py:30
  244.4 3.0 copy.73
  247.5 43.7 %reduce-scatter.2.cloned.1.call-done = f32[1024,128]{0,1:T(8,128)} async-done(((f32[4096,128]{0,1:T(8,128)}), f32[1024,128]{0,1:T(8,128)}) %reduce-scatter.2.cloned.1.call-update) | async-done | bytes 524304 | tf_op jit(solution)/shard_map/reduce_scatter | solution.py:57
  (71 shorter events, 11.1 us)
Async XLA Ops:
  7.2 42.0 %all-gather.2.cloned.1.call-start = ((), (), s32[]{:S(2)}) async-start(), calls=%async_computation.1 | async-start | bytes 4718592 | tf_op jit(solution)/shard_map/all_gather | solution.py:56
  7.9 283.3 %reduce-scatter.2.cloned.1.call-start = ((), (), s32[]{:S(2)}) async-start(), calls=%async_computation.2 | async-start | bytes 2621440 | tf_op jit(solution)/shard_map/reduce_scatter | solution.py:57
  244.4 46.7 %copy-start = (s32[4,1024]{1,0:T(4,128)S(1)}, s32[4,1024]{1,0:T(4,128)}, u32[]{:S(2)}) copy-start(s32[4,1024]{1,0:T(4,128)} %param.9) | copy-start | bytes 49156
Sparse Core Ops, SparseCore 0:
  9.9 39.2 all-gather.1
  247.5 43.5 reduce-scatter.1
where the time goes:
time: 303 us
  matrix products  97.5 us (32%)
  waiting for transfers between devices  85.6 us (28%)
  other arithmetic  74.2 us (24%)
  local copies, waits for them, and re-layouts  30 us (10%)
  between operations  14.1 us (5%)
    dot_general x16, matrix products, add_block(): jnp.dot(expand_bits(packed_cols), vector_rows, preferred_element_type=jnp...  97.5 us
    convert_element_type x16, other arithmetic, expand_bits(): bit_table.reshape(packed.shape[0], packed.shape[1] * 32)  70.8 us
    reduce_scatter x1, waiting for transfers between devices, shards(): lax.psum_scatter(partial_sum, 'row', scatter_dimension=0, tiled=True)  43.7 us
    all_gather x1, waiting for transfers between devices, shards(): lax.all_gather(frontier, 'col', axis=0, tiled=True)  41.2 us
    dynamic_slice x8, local copies, waits for them, and re-layouts, tile_product(): return lax.map(one_rows, row_blocks).reshape(row_total, vectors.shape[1])  20.1 us
  transfers between devices with their start and end apart: 2, of which 2 were waited for; matrix products, arithmetic and copies ran while one was open for 0% of the time, Pallas kernels for 0%

commit v1 on v0

--- a/solution.py
+++ b/solution.py
@@ -4,6 +4,11 @@
 import jax.numpy as jnp
 from jax import lax
 from jax.sharding import PartitionSpec as P
+
+
+def all_by_exchange(x, axis, d):
+    repeated = jnp.stack([x] * lax.axis_size(axis))
+    return jnp.concatenate(lax.all_to_all(repeated, axis, 0, 0), axis=d)
 
 
 def expand_bits(packed):
@@ -53,7 +58,7 @@
 
 
 def shards(adjacency, frontier, visited):
-    partial_sum = tile_product(adjacency, lax.all_gather(frontier, "col", axis=0, tiled=True))
+    partial_sum = tile_product(adjacency, all_by_exchange(frontier, "col", 0))
     reached = lax.psum_scatter(partial_sum, "row", scatter_dimension=0, tiled=True)
     return finish(reached, visited)
 

time: 303 us -> 319 us (1.053)
  waiting for transfers between devices: 85.6 us -> 93 us
  starting transfers between devices: 0.08 us -> 5.23 us
  local copies, waits for them, and re-layouts: 30 us -> 33.5 us
    all_to_all x0 -> x1, waiting for transfers between devices: none -> 49.1 us  [all_by_exchange(): return jnp.concatenate(lax.all_to_all(repeated, axis, 0, 0), axis=d)]
    all_gather x1 -> x0, waiting for transfers between devices: 41.2 us -> none  [shards(): lax.all_gather(frontier, 'col', axis=0, tiled=True)]
    all_to_all x0 -> x1, starting transfers between devices: none -> 5.2 us  [all_by_exchange(): return jnp.concatenate(lax.all_to_all(repeated, axis, 0, 0), axis=d)]
    another operation x0 -> x1, local copies, waits for them, and re-layouts: none -> 3.52 us  [all_by_exchange(): repeated = jnp.stack([x] * lax.axis_size(axis))]
where the time goes in v1:
time: 319 us
  matrix products  97.5 us (31%)
  waiting for transfers between devices  93 us (29%)
  other arithmetic  74.4 us (23%)
  local copies, waits for them, and re-layouts  33.5 us (11%)
  between operations  14.1 us (4%)
  starting transfers between devices  5.23 us (2%)
    dot_general x16, matrix products, add_block(): jnp.dot(expand_bits(packed_cols), vector_rows, preferred_element_type=jnp...  97.5 us
    convert_element_type x16, other arithmetic, expand_bits(): bit_table.reshape(packed.shape[0], packed.shape[1] * 32)  71 us
    all_to_all x1, waiting for transfers between devices, all_by_exchange(): return jnp.concatenate(lax.all_to_all(repeated, axis, 0, 0), axis=d)  49.1 us
    reduce_scatter x1, waiting for transfers between devices, shards(): lax.psum_scatter(partial_sum, 'row', scatter_dimension=0, tiled=True)  43.9 us
    dynamic_slice x8, local copies, waits for them, and re-layouts, tile_product(): return lax.map(one_rows, row_blocks).reshape(row_total, vectors.shape[1])  20.1 us
  transfers between devices with their start and end apart: 2, of which 2 were waited for; matrix products, arithmetic and copies ran while one was open for 0% of the time, Pallas kernels for 0%

profile of v1, /device:TPU:0, one launch (start us, length us, event | category | flops | bytes accessed | tf_op | source)
XLA Modules:
  0.0 318.8 jit_solution(8991759900233269007)
XLA Ops:
  7.2 3.5 %stack.2 = bf16[8,2048,128]{2,1,0:T(8,128)(2,1)} broadcast(bf16[2048,128]{1,0:T(8,128)(2,1)} %param.8), dimensions={1,2} | broadcast | bytes 4718592 | tf_op jit(solution)/shard_map/stack | solution.py:10
  10.7 5.2 %all-to-all-start = ((bf16[8,2048,128]{2,1,0:T(8,128)(2,1)}), bf16[8,2048,128]{2,1,0:T(8,128)(2,1)}, u32[]{:S(2)}, u32[]{:S(2)}) async-start(bf16[8,2048,128]{2,1,0:T(8,128)(2,1)} %stack.2), calls=%async_computation | async-start | bytes 8388608 | tf_op jit(solution)/shard_map/all_to_all | solution.py:11
  15.9 49.1 %all-to-all-done = bf16[8,2048,128]{2,1,0:T(8,128)(2,1)} async-done(((bf16[8,2048,128]{2,1,0:T(8,128)(2,1)}), bf16[8,2048,128]{2,1,0:T(8,128)(2,1)}, u32[]{:S(2)}, u32[]{:S(2)}) %all-to-all-start) | async-done | bytes 4194336 | tf_op jit(solution)/shard_map/all_to_all | solution.py:11
  65.1 195.4 %while.36 = (s32[]{:T(128)}, f32[4,1024,128]{2,1,0:T(8,128)}, s32[4,1024,512]{2,1,0:T(8,128)}, bf16[16384,128]{1,0:T(8,128)(2,1)}, s32[]{:T(128)}, /*index=5*/s3...) while((s32[]{:T(128)}, f32[4,1024,128]{2,1,0:T(8,128)}, ...), condition=%wide.region_3.4_spmd, body=%wide.region_0.3_spmd.sunk | while | flops 1086586880 | bytes 29951060 | solution.py:41
  65.1 3.1 constant_dynamic-slice_fusion.4
  68.2 1.9 copy.298
  70.1 43.0 %while.37 = (s32[]{:T(128)}, f32[1024,128]{1,0:T(8,128)S(1)}, s32[1024,512]{0,1:T(8,128)S(1)}, bf16[16384,128]{1,0:T(8,128)(2,1)}, s32[]{:T(128)}, /*index=5*/s3...) while((s32[]{:T(128)}, f32[1024,128]{1,0:T(8,128)S(1)}, ...), condition=%wide.region_2.2_spmd.clone, body=%wide.region_1.1_spmd.clone.sunk | while | flops 1086586880 | bytes 20513124 | solution.py:39
  70.3 4.4 %fusion.66 = bf16[1024,4096]{0,1:T(8,128)(2,1)} fusion(s32[4096]{0:T(1024)S(1)} %shift_right_arithmetic.108, s32[1024,128]{0,1:T(8,128)S(1)} %constant_dynamic-slice_fusion.5), kind=kLoop, calls=%fused_computation.2.clone.1 | loop fusion | flops 12582912 | bytes 8929280 | tf_op jit(solution)/shard_map/while/body/eval_jaxpr/while/body/eval_jaxpr/convert_element_type | solution.py:17
  74.8 6.1 %convolution_add_fusion.2 = f32[1024,128]{1,0:T(8,128)S(1)} fusion(bf16[1024,4096]{0,1:T(8,128)(2,1)} %fusion.66, bf16[16384,128]{1,0:T(8,128)(2,1)} %get-tuple-element.340, s32[]{:T(128)S(6)} %select_n.46, f32[1024,128]{1,0:T(8,128)S(1)} %get-tuple-element.326, pred[]{:T(512)S(6)} %compare.13), kind=kOutput, calls=%fused_computation.3.clone.1 | convolution fusion | flops 1074003968 | bytes 10485765 | tf_op jit(solution)/shard_map/while/body/eval_jaxpr/while/body/eval_jaxpr/dot_general | solution.py:35
  81.1 4.4 %fusion.66 = bf16[1024,4096]{0,1:T(8,128)(2,1)} fusion(s32[4096]{0:T(1024)S(1)} %shift_right_arithmetic.108, s32[1024,128]{0,1:T(8,128)S(1)} %constant_dynamic-slice_fusion.5), kind=kLoop, calls=%fused_computation.2.clone.1 | loop fusion | flops 12582912 | bytes 8929280 | tf_op jit(solution)/shard_map/while/body/eval_jaxpr/while/body/eval_jaxpr/convert_element_type | solution.py:17
  85.5 6.1 %convolution_add_fusion.2 = f32[1024,128]{1,0:T(8,128)S(1)} fusion(bf16[1024,4096]{0,1:T(8,128)(2,1)} %fusion.66, bf16[16384,128]{1,0:T(8,128)(2,1)} %get-tuple-element.340, s32[]{:T(128)S(6)} %select_n.46, f32[1024,128]{1,0:T(8,128)S(1)} %get-tuple-element.326, pred[]{:T(512)S(6)} %compare.13), kind=kOutput, calls=%fused_computation.3.clone.1 | convolution fusion | flops 1074003968 | bytes 10485765 | tf_op jit(solution)/shard_map/while/body/eval_jaxpr/while/body/eval_jaxpr/dot_general | solution.py:35
  91.8 4.4 %fusion.66 = bf16[1024,4096]{0,1:T(8,128)(2,1)} fusion(s32[4096]{0:T(1024)S(1)} %shift_right_arithmetic.108, s32[1024,128]{0,1:T(8,128)S(1)} %constant_dynamic-slice_fusion.5), kind=kLoop, calls=%fused_computation.2.clone.1 | loop fusion | flops 12582912 | bytes 8929280 | tf_op jit(solution)/shard_map/while/body/eval_jaxpr/while/body/eval_jaxpr/convert_element_type | solution.py:17
  96.2 6.1 %convolution_add_fusion.2 = f32[1024,128]{1,0:T(8,128)S(1)} fusion(bf16[1024,4096]{0,1:T(8,128)(2,1)} %fusion.66, bf16[16384,128]{1,0:T(8,128)(2,1)} %get-tuple-element.340, s32[]{:T(128)S(6)} %select_n.46, f32[1024,128]{1,0:T(8,128)S(1)} %get-tuple-element.326, pred[]{:T(512)S(6)} %compare.13), kind=kOutput, calls=%fused_computation.3.clone.1 | convolution fusion | flops 1074003968 | bytes 10485765 | tf_op jit(solution)/shard_map/while/body/eval_jaxpr/while/body/eval_jaxpr/dot_general | solution.py:35
  102.5 4.4 %fusion.66 = bf16[1024,4096]{0,1:T(8,128)(2,1)} fusion(s32[4096]{0:T(1024)S(1)} %shift_right_arithmetic.108, s32[1024,128]{0,1:T(8,128)S(1)} %constant_dynamic-slice_fusion.5), kind=kLoop, calls=%fused_computation.2.clone.1 | loop fusion | flops 12582912 | bytes 8929280 | tf_op jit(solution)/shard_map/while/body/eval_jaxpr/while/body/eval_jaxpr/convert_element_type | solution.py:17
  107.0 6.1 %convolution_add_fusion.2 = f32[1024,128]{1,0:T(8,128)S(1)} fusion(bf16[1024,4096]{0,1:T(8,128)(2,1)} %fusion.66, bf16[16384,128]{1,0:T(8,128)(2,1)} %get-tuple-element.340, s32[]{:T(128)S(6)} %select_n.46, f32[1024,128]{1,0:T(8,128)S(1)} %get-tuple-element.326, pred[]{:T(512)S(6)} %compare.13), kind=kOutput, calls=%fused_computation.3.clone.1 | convolution fusion | flops 1074003968 | bytes 10485765 | tf_op jit(solution)/shard_map/while/body/eval_jaxpr/while/body/eval_jaxpr/dot_general | solution.py:35
  113.9 3.1 constant_dynamic-slice_fusion.4
  117.1 1.9 copy.298
  119.0 43.0 %while.37 = (s32[]{:T(128)}, f32[1024,128]{1,0:T(8,128)S(1)}, s32[1024,512]{0,1:T(8,128)S(1)}, bf16[16384,128]{1,0:T(8,128)(2,1)}, s32[]{:T(128)}, /*index=5*/s3...) while((s32[]{:T(128)}, f32[1024,128]{1,0:T(8,128)S(1)}, ...), condition=%wide.region_2.2_spmd.clone, body=%wide.region_1.1_spmd.clone.sunk | while | flops 1086586880 | bytes 20513124 | solution.py:39
  119.2 4.4 %fusion.66 = bf16[1024,4096]{0,1:T(8,128)(2,1)} fusion(s32[4096]{0:T(1024)S(1)} %shift_right_arithmetic.108, s32[1024,128]{0,1:T(8,128)S(1)} %constant_dynamic-slice_fusion.5), kind=kLoop, calls=%fused_computation.2.clone.1 | loop fusion | flops 12582912 | bytes 8929280 | tf_op jit(solution)/shard_map/while/body/eval_jaxpr/while/body/eval_jaxpr/convert_element_type | solution.py:17
  123.6 6.1 %convolution_add_fusion.2 = f32[1024,128]{1,0:T(8,128)S(1)} fusion(bf16[1024,4096]{0,1:T(8,128)(2,1)} %fusion.66, bf16[16384,128]{1,0:T(8,128)(2,1)} %get-tuple-element.340, s32[]{:T(128)S(6)} %select_n.46, f32[1024,128]{1,0:T(8,128)S(1)} %get-tuple-element.326, pred[]{:T(512)S(6)} %compare.13), kind=kOutput, calls=%fused_computation.3.clone.1 | convolution fusion | flops 1074003968 | bytes 10485765 | tf_op jit(solution)/shard_map/while/body/eval_jaxpr/while/body/eval_jaxpr/dot_general | solution.py:35
  129.9 4.4 %fusion.66 = bf16[1024,4096]{0,1:T(8,128)(2,1)} fusion(s32[4096]{0:T(1024)S(1)} %shift_right_arithmetic.108, s32[1024,128]{0,1:T(8,128)S(1)} %constant_dynamic-slice_fusion.5), kind=kLoop, calls=%fused_computation.2.clone.1 | loop fusion | flops 12582912 | bytes 8929280 | tf_op jit(solution)/shard_map/while/body/eval_jaxpr/while/body/eval_jaxpr/convert_element_type | solution.py:17
  134.4 6.1 %convolution_add_fusion.2 = f32[1024,128]{1,0:T(8,128)S(1)} fusion(bf16[1024,4096]{0,1:T(8,128)(2,1)} %fusion.66, bf16[16384,128]{1,0:T(8,128)(2,1)} %get-tuple-element.340, s32[]{:T(128)S(6)} %select_n.46, f32[1024,128]{1,0:T(8,128)S(1)} %get-tuple-element.326, pred[]{:T(512)S(6)} %compare.13), kind=kOutput, calls=%fused_computation.3.clone.1 | convolution fusion | flops 1074003968 | bytes 10485765 | tf_op jit(solution)/shard_map/while/body/eval_jaxpr/while/body/eval_jaxpr/dot_general | solution.py:35
  140.7 4.4 %fusion.66 = bf16[1024,4096]{0,1:T(8,128)(2,1)} fusion(s32[4096]{0:T(1024)S(1)} %shift_right_arithmetic.108, s32[1024,128]{0,1:T(8,128)S(1)} %constant_dynamic-slice_fusion.5), kind=kLoop, calls=%fused_computation.2.clone.1 | loop fusion | flops 12582912 | bytes 8929280 | tf_op jit(solution)/shard_map/while/body/eval_jaxpr/while/body/eval_jaxpr/convert_element_type | solution.py:17
  145.1 6.1 %convolution_add_fusion.2 = f32[1024,128]{1,0:T(8,128)S(1)} fusion(bf16[1024,4096]{0,1:T(8,128)(2,1)} %fusion.66, bf16[16384,128]{1,0:T(8,128)(2,1)} %get-tuple-element.340, s32[]{:T(128)S(6)} %select_n.46, f32[1024,128]{1,0:T(8,128)S(1)} %get-tuple-element.326, pred[]{:T(512)S(6)} %compare.13), kind=kOutput, calls=%fused_computation.3.clone.1 | convolution fusion | flops 1074003968 | bytes 10485765 | tf_op jit(solution)/shard_map/while/body/eval_jaxpr/while/body/eval_jaxpr/dot_general | solution.py:35
  151.4 4.4 %fusion.66 = bf16[1024,4096]{0,1:T(8,128)(2,1)} fusion(s32[4096]{0:T(1024)S(1)} %shift_right_arithmetic.108, s32[1024,128]{0,1:T(8,128)S(1)} %constant_dynamic-slice_fusion.5), kind=kLoop, calls=%fused_computation.2.clone.1 | loop fusion | flops 12582912 | bytes 8929280 | tf_op jit(solution)/shard_map/while/body/eval_jaxpr/while/body/eval_jaxpr/convert_element_type | solution.py:17
  155.8 6.1 %convolution_add_fusion.2 = f32[1024,128]{1,0:T(8,128)S(1)} fusion(bf16[1024,4096]{0,1:T(8,128)(2,1)} %fusion.66, bf16[16384,128]{1,0:T(8,128)(2,1)} %get-tuple-element.340, s32[]{:T(128)S(6)} %select_n.46, f32[1024,128]{1,0:T(8,128)S(1)} %get-tuple-element.326, pred[]{:T(512)S(6)} %compare.13), kind=kOutput, calls=%fused_computation.3.clone.1 | convolution fusion | flops 1074003968 | bytes 10485765 | tf_op jit(solution)/shard_map/while/body/eval_jaxpr/while/body/eval_jaxpr/dot_general | solution.py:35
  162.8 3.1 constant_dynamic-slice_fusion.4
  167.9 43.0 %while.37 = (s32[]{:T(128)}, f32[1024,128]{1,0:T(8,128)S(1)}, s32[1024,512]{0,1:T(8,128)S(1)}, bf16[16384,128]{1,0:T(8,128)(2,1)}, s32[]{:T(128)}, /*index=5*/s3...) while((s32[]{:T(128)}, f32[1024,128]{1,0:T(8,128)S(1)}, ...), condition=%wide.region_2.2_spmd.clone, body=%wide.region_1.1_spmd.clone.sunk | while | flops 1086586880 | bytes 20513124 | solution.py:39
  168.1 4.4 %fusion.66 = bf16[1024,4096]{0,1:T(8,128)(2,1)} fusion(s32[4096]{0:T(1024)S(1)} %shift_right_arithmetic.108, s32[1024,128]{0,1:T(8,128)S(1)} %constant_dynamic-slice_fusion.5), kind=kLoop, calls=%fused_computation.2.clone.1 | loop fusion | flops 12582912 | bytes 8929280 | tf_op jit(solution)/shard_map/while/body/eval_jaxpr/while/body/eval_jaxpr/convert_element_type | solution.py:17
  172.5 6.1 %convolution_add_fusion.2 = f32[1024,128]{1,0:T(8,128)S(1)} fusion(bf16[1024,4096]{0,1:T(8,128)(2,1)} %fusion.66, bf16[16384,128]{1,0:T(8,128)(2,1)} %get-tuple-element.340, s32[]{:T(128)S(6)} %select_n.46, f32[1024,128]{1,0:T(8,128)S(1)} %get-tuple-element.326, pred[]{:T(512)S(6)} %compare.13), kind=kOutput, calls=%fused_computation.3.clone.1 | convolution fusion | flops 1074003968 | bytes 10485765 | tf_op jit(solution)/shard_map/while/body/eval_jaxpr/while/body/eval_jaxpr/dot_general | solution.py:35
  178.8 4.4 %fusion.66 = bf16[1024,4096]{0,1:T(8,128)(2,1)} fusion(s32[4096]{0:T(1024)S(1)} %shift_right_arithmetic.108, s32[1024,128]{0,1:T(8,128)S(1)} %constant_dynamic-slice_fusion.5), kind=kLoop, calls=%fused_computation.2.clone.1 | loop fusion | flops 12582912 | bytes 8929280 | tf_op jit(solution)/shard_map/while/body/eval_jaxpr/while/body/eval_jaxpr/convert_element_type | solution.py:17
  183.2 6.1 %convolution_add_fusion.2 = f32[1024,128]{1,0:T(8,128)S(1)} fusion(bf16[1024,4096]{0,1:T(8,128)(2,1)} %fusion.66, bf16[16384,128]{1,0:T(8,128)(2,1)} %get-tuple-element.340, s32[]{:T(128)S(6)} %select_n.46, f32[1024,128]{1,0:T(8,128)S(1)} %get-tuple-element.326, pred[]{:T(512)S(6)} %compare.13), kind=kOutput, calls=%fused_computation.3.clone.1 | convolution fusion | flops 1074003968 | bytes 10485765 | tf_op jit(solution)/shard_map/while/body/eval_jaxpr/while/body/eval_jaxpr/dot_general | solution.py:35
  189.5 4.4 %fusion.66 = bf16[1024,4096]{0,1:T(8,128)(2,1)} fusion(s32[4096]{0:T(1024)S(1)} %shift_right_arithmetic.108, s32[1024,128]{0,1:T(8,128)S(1)} %constant_dynamic-slice_fusion.5), kind=kLoop, calls=%fused_computation.2.clone.1 | loop fusion | flops 12582912 | bytes 8929280 | tf_op jit(solution)/shard_map/while/body/eval_jaxpr/while/body/eval_jaxpr/convert_element_type | solution.py:17
  194.0 6.1 %convolution_add_fusion.2 = f32[1024,128]{1,0:T(8,128)S(1)} fusion(bf16[1024,4096]{0,1:T(8,128)(2,1)} %fusion.66, bf16[16384,128]{1,0:T(8,128)(2,1)} %get-tuple-element.340, s32[]{:T(128)S(6)} %select_n.46, f32[1024,128]{1,0:T(8,128)S(1)} %get-tuple-element.326, pred[]{:T(512)S(6)} %compare.13), kind=kOutput, calls=%fused_computation.3.clone.1 | convolution fusion | flops 1074003968 | bytes 10485765 | tf_op jit(solution)/shard_map/while/body/eval_jaxpr/while/body/eval_jaxpr/dot_general | solution.py:35
  200.3 4.4 %fusion.66 = bf16[1024,4096]{0,1:T(8,128)(2,1)} fusion(s32[4096]{0:T(1024)S(1)} %shift_right_arithmetic.108, s32[1024,128]{0,1:T(8,128)S(1)} %constant_dynamic-slice_fusion.5), kind=kLoop, calls=%fused_computation.2.clone.1 | loop fusion | flops 12582912 | bytes 8929280 | tf_op jit(solution)/shard_map/while/body/eval_jaxpr/while/body/eval_jaxpr/convert_element_type | solution.py:17
  204.7 6.1 %convolution_add_fusion.2 = f32[1024,128]{1,0:T(8,128)S(1)} fusion(bf16[1024,4096]{0,1:T(8,128)(2,1)} %fusion.66, bf16[16384,128]{1,0:T(8,128)(2,1)} %get-tuple-element.340, s32[]{:T(128)S(6)} %select_n.46, f32[1024,128]{1,0:T(8,128)S(1)} %get-tuple-element.326, pred[]{:T(512)S(6)} %compare.13), kind=kOutput, calls=%fused_computation.3.clone.1 | convolution fusion | flops 1074003968 | bytes 10485765 | tf_op jit(solution)/shard_map/while/body/eval_jaxpr/while/body/eval_jaxpr/dot_general | solution.py:35
  211.7 3.1 constant_dynamic-slice_fusion.4
  216.7 43.0 %while.37 = (s32[]{:T(128)}, f32[1024,128]{1,0:T(8,128)S(1)}, s32[1024,512]{0,1:T(8,128)S(1)}, bf16[16384,128]{1,0:T(8,128)(2,1)}, s32[]{:T(128)}, /*index=5*/s3...) while((s32[]{:T(128)}, f32[1024,128]{1,0:T(8,128)S(1)}, ...), condition=%wide.region_2.2_spmd.clone, body=%wide.region_1.1_spmd.clone.sunk | while | flops 1086586880 | bytes 20513124 | solution.py:39
  216.9 4.4 %fusion.66 = bf16[1024,4096]{0,1:T(8,128)(2,1)} fusion(s32[4096]{0:T(1024)S(1)} %shift_right_arithmetic.108, s32[1024,128]{0,1:T(8,128)S(1)} %constant_dynamic-slice_fusion.5), kind=kLoop, calls=%fused_computation.2.clone.1 | loop fusion | flops 12582912 | bytes 8929280 | tf_op jit(solution)/shard_map/while/body/eval_jaxpr/while/body/eval_jaxpr/convert_element_type | solution.py:17
  221.3 6.1 %convolution_add_fusion.2 = f32[1024,128]{1,0:T(8,128)S(1)} fusion(bf16[1024,4096]{0,1:T(8,128)(2,1)} %fusion.66, bf16[16384,128]{1,0:T(8,128)(2,1)} %get-tuple-element.340, s32[]{:T(128)S(6)} %select_n.46, f32[1024,128]{1,0:T(8,128)S(1)} %get-tuple-element.326, pred[]{:T(512)S(6)} %compare.13), kind=kOutput, calls=%fused_computation.3.clone.1 | convolution fusion | flops 1074003968 | bytes 10485765 | tf_op jit(solution)/shard_map/while/body/eval_jaxpr/while/body/eval_jaxpr/dot_general | solution.py:35
  227.6 4.4 %fusion.66 = bf16[1024,4096]{0,1:T(8,128)(2,1)} fusion(s32[4096]{0:T(1024)S(1)} %shift_right_arithmetic.108, s32[1024,128]{0,1:T(8,128)S(1)} %constant_dynamic-slice_fusion.5), kind=kLoop, calls=%fused_computation.2.clone.1 | loop fusion | flops 12582912 | bytes 8929280 | tf_op jit(solution)/shard_map/while/body/eval_jaxpr/while/body/eval_jaxpr/convert_element_type | solution.py:17
  232.1 6.1 %convolution_add_fusion.2 = f32[1024,128]{1,0:T(8,128)S(1)} fusion(bf16[1024,4096]{0,1:T(8,128)(2,1)} %fusion.66, bf16[16384,128]{1,0:T(8,128)(2,1)} %get-tuple-element.340, s32[]{:T(128)S(6)} %select_n.46, f32[1024,128]{1,0:T(8,128)S(1)} %get-tuple-element.326, pred[]{:T(512)S(6)} %compare.13), kind=kOutput, calls=%fused_computation.3.clone.1 | convolution fusion | flops 1074003968 | bytes 10485765 | tf_op jit(solution)/shard_map/while/body/eval_jaxpr/while/body/eval_jaxpr/dot_general | solution.py:35
  238.4 4.4 %fusion.66 = bf16[1024,4096]{0,1:T(8,128)(2,1)} fusion(s32[4096]{0:T(1024)S(1)} %shift_right_arithmetic.108, s32[1024,128]{0,1:T(8,128)S(1)} %constant_dynamic-slice_fusion.5), kind=kLoop, calls=%fused_computation.2.clone.1 | loop fusion | flops 12582912 | bytes 8929280 | tf_op jit(solution)/shard_map/while/body/eval_jaxpr/while/body/eval_jaxpr/convert_element_type | solution.py:17
  242.8 6.1 %convolution_add_fusion.2 = f32[1024,128]{1,0:T(8,128)S(1)} fusion(bf16[1024,4096]{0,1:T(8,128)(2,1)} %fusion.66, bf16[16384,128]{1,0:T(8,128)(2,1)} %get-tuple-element.340, s32[]{:T(128)S(6)} %select_n.46, f32[1024,128]{1,0:T(8,128)S(1)} %get-tuple-element.326, pred[]{:T(512)S(6)} %compare.13), kind=kOutput, calls=%fused_computation.3.clone.1 | convolution fusion | flops 1074003968 | bytes 10485765 | tf_op jit(solution)/shard_map/while/body/eval_jaxpr/while/body/eval_jaxpr/dot_general | solution.py:35
  249.1 4.4 %fusion.66 = bf16[1024,4096]{0,1:T(8,128)(2,1)} fusion(s32[4096]{0:T(1024)S(1)} %shift_right_arithmetic.108, s32[1024,128]{0,1:T(8,128)S(1)} %constant_dynamic-slice_fusion.5), kind=kLoop, calls=%fused_computation.2.clone.1 | loop fusion | flops 12582912 | bytes 8929280 | tf_op jit(solution)/shard_map/while/body/eval_jaxpr/while/body/eval_jaxpr/convert_element_type | solution.py:17
  253.6 6.1 %convolution_add_fusion.2 = f32[1024,128]{1,0:T(8,128)S(1)} fusion(bf16[1024,4096]{0,1:T(8,128)(2,1)} %fusion.66, bf16[16384,128]{1,0:T(8,128)(2,1)} %get-tuple-element.340, s32[]{:T(128)S(6)} %select_n.46, f32[1024,128]{1,0:T(8,128)S(1)} %get-tuple-element.326, pred[]{:T(512)S(6)} %compare.13), kind=kOutput, calls=%fused_computation.3.clone.1 | convolution fusion | flops 1074003968 | bytes 10485765 | tf_op jit(solution)/shard_map/while/body/eval_jaxpr/while/body/eval_jaxpr/dot_general | solution.py:35
  260.5 2.9 copy.73
  263.5 43.9 %reduce-scatter.2.cloned.1.call-done = f32[1024,128]{0,1:T(8,128)} async-done(((f32[4096,128]{0,1:T(8,128)}), f32[1024,128]{0,1:T(8,128)}) %reduce-scatter.2.cloned.1.call-update) | async-done | bytes 524304 | tf_op jit(solution)/shard_map/reduce_scatter | solution.py:62
  (71 shorter events, 14.2 us)
Async XLA Ops:
  10.7 54.4 %all-to-all-start = ((bf16[8,2048,128]{2,1,0:T(8,128)(2,1)}), bf16[8,2048,128]{2,1,0:T(8,128)(2,1)}, u32[]{:S(2)}, u32[]{:S(2)}) async-start(bf16[8,2048,128]{2,1,0:T(8,128)(2,1)} %stack.2), calls=%async_computation | async-start | bytes 8388608 | tf_op jit(solution)/shard_map/all_to_all | solution.py:11
  15.9 291.5 %reduce-scatter.2.cloned.1.call-start = ((), (), s32[]{:S(2)}) async-start(), calls=%async_computation.2 | async-start | bytes 2621440 | tf_op jit(solution)/shard_map/reduce_scatter | solution.py:62
  260.5 46.9 %copy-start = (s32[4,1024]{1,0:T(4,128)S(1)}, s32[4,1024]{1,0:T(4,128)}, u32[]{:S(2)}) copy-start(s32[4,1024]{1,0:T(4,128)} %param.9) | copy-start | bytes 49156
Sparse Core Ops, SparseCore 0:
  263.6 43.7 reduce-scatter.1
